TPU v7x, 32 devices: a whole 2x2x4 slice. The times are simulated.
32 devices in a mesh: grp: 2 (over y), row: 4 (over x, core), col: 4 (over z).
Axes of the slice: x: 2, y: 2, z: 4, core: 2. Of those that a mesh axis runs over, the one named last changes fastest.
Arguments:
- perturbation: bfloat16 [4, 12000, 12000], P('grp', 'row', 'col'), parts along dimension 0, may hold values from -96 to 96
- occ_coeffs: bfloat16 [12000, 2000], P('row', 'col'), may hold values from -0.0546875 to 0.0546875
- vir_coeffs: bfloat16 [12000, 512], P('col', 'row'), may hold values from -0.0546875 to 0.0546875
- occ_energies: float32 [2000], replicated, may hold values from -1 to -0.1
- vir_energies: float32 [512], replicated, may hold values from 0.1 to 1.5
Outputs:
- density_response: bfloat16 [4, 12000, 12000], P('grp', 'row', 'col'), parts along dimension 0
There are 2 independent parts, one for each index of `grp`. A program takes and returns all parts, laid end to end along the dimension named above; an argument that names none is the same for every part. Nothing has to cross between parts.
All inputs are finite; a program needn't handle non-finite values.
Results may differ from a plain program's by a relative error of at most 0.0098.
Values may be sent and summed in bfloat16 or wider, within the bound.
A program may use at most 192 MiB of HBM per device.

v0:
```python
import jax
import jax.numpy as jnp
from jax import lax
from jax.sharding import PartitionSpec as P

BF16 = jnp.bfloat16
F32 = jnp.float32


def per_device(perturbation, occ_coeffs, vir_coeffs, occ_energies, vir_energies):
    vir_rows = lax.all_gather(vir_coeffs, "row", axis=1, tiled=True)
    occ_parts = lax.all_gather(occ_coeffs, "col")
    cols, _, width = occ_parts.shape
    image = jnp.einsum("pij,jv->piv", perturbation, vir_rows, preferred_element_type=F32).astype(
        BF16
    )
    part = jnp.einsum("cio,piv->pcov", occ_parts, image, preferred_element_type=F32).astype(BF16)
    coupling = lax.psum(part, ("row", "col"))
    gaps = occ_energies.reshape(cols, width)[:, :, None] - vir_energies[None, None, :]
    response = (coupling.astype(F32) / gaps[None]).astype(BF16)
    mixed = jnp.einsum("cio,pcov->piv", occ_parts, response, preferred_element_type=F32).astype(
        BF16
    )
    return jnp.einsum("piv,jv->pij", mixed, vir_rows, preferred_element_type=F32).astype(BF16)


def solution(mesh):
    placed = (P("grp", "row", "col"), P("row", "col"), P("col", "row"), P(), P())
    return jax.shard_map(
        per_device, mesh=mesh, in_specs=placed, out_specs=P("grp", "row", "col"), check_vma=False
    )
```

profile of v0, /device:TPU:0, one launch (start us, length us, event | category | flops | bytes accessed | tf_op | source)
XLA Modules:
  0.0 448.0 jit_solution(10581064769501468559)
XLA Ops:
  6.5 0.0 all-gather.4.cloned.1.call-start
  6.5 0.7 all-gather.4.cloned.1.call-update
  7.3 0.0 all-gather.6.cloned.1.call-start
  7.3 0.7 all-gather.6.cloned.1.call-update
  8.0 0.0 all-reduce.2.cloned.1.call-start
  8.1 32.1 %all-gather.4.cloned.1.call-done = bf16[3000,512]{1,0:T(8,128)(2,1)} async-done(((bf16[3000,128]{1,0:T(8,128)(2,1)}), bf16[3000,512]{1,0:T(8,128)(2,1)}) %all-gather.4.cloned.1.call-update) | async-done | bytes 3072016 | tf_op jit(solution)/shard_map/all_gather | solution.py:11
  40.1 25.8 %fusion.45 = bf16[2,3000,512,1]{2,1,3,0:T(8,128)(2,1)} fusion(bf16[2,3000,3000]{2,1,0:T(8,128)(2,1)} %param.5, bf16[3000,512]{1,0:T(8,128)(2,1)} %all-gather.4.cloned.1.call-done), kind=kOutput, calls=%fused_computation.5.clone.clone.clone.1 | convolution fusion | flops 18435072000 | bytes 45216000 | tf_op jit(solution)/shard_map/pij,jv->piv/dot_general | solution.py:14
  66.0 189.1 %all-gather.6.cloned.1.call-done = bf16[12000,500]{1,0:T(8,128)(2,1)} async-done(((bf16[3000,500]{1,0:T(8,128)(2,1)}), bf16[12000,500]{1,0:T(8,128)(2,1)}) %all-gather.6.cloned.1.call-update) | async-done | bytes 12000016 | tf_op jit(solution)/shard_map/all_gather | solution.py:12
  255.1 19.1 %fusion.17 = bf16[2,512,4,500]{1,3,2,0:T(8,128)(2,1)} fusion(bf16[4,3000,500,1]{2,1,0,3:T(8,128)(2,1)} %bitcast.58, bf16[2,3000,512,1]{2,1,3,0:T(8,128)(2,1)} %fusion.45), kind=kOutput, calls=%fused_computation.12 | convolution fusion | flops 12290048000 | bytes 22240000 | tf_op jit(solution)/shard_map/cio,piv->pcov/dot_general | solution.py:17
  274.2 0.0 copy-start
  274.2 0.0 copy-start.1
  274.2 7.8 %copy.10 = bf16[2,512,4,500]{3,2,1,0:T(4,128)(2,1)} copy(bf16[2,512,4,500]{1,3,2,0:T(8,128)(2,1)} %fusion.17) | data formatting | bytes 8192000
  282.0 0.0 all-reduce.2.cloned.1.call-update
  282.0 0.0 copy-done
  282.1 0.1 sub.19
  282.1 0.0 copy-done.1
  282.1 2.8 broadcast_subtract_fusion
  285.0 106.6 %all-reduce.2.cloned.1.call-done = bf16[2,4,500,512]{2,1,3,0:T(4,128)(2,1)} async-done(((bf16[2,4,500,512]{2,1,3,0:T(4,128)(2,1)}), bf16[2,4,500,512]{2,1,3,0:T(4,128)(2,1)}) %all-reduce.2.cloned.1.call-update) | async-done | bytes 4096016 | tf_op jit(solution)/shard_map/psum | solution.py:18
  391.5 5.5 %fusion = bf16[2,4,500,512]{2,1,3,0:T(4,128)(2,1)S(1)} fusion(bf16[2,4,500,512]{2,1,3,0:T(4,128)(2,1)} %all-reduce.2.cloned.1.call-done, f32[4,500,512]{1,0,2:T(4,128)} %broadcast_subtract_fusion), kind=kLoop, calls=%fused_computation.3 | loop fusion | flops 6144000 | bytes 12288000 | tf_op jit(solution)/shard_map/convert_element_type | solution.py:20
  397.1 16.8 %fusion.41 = bf16[2,3000,512]{2,1,0:T(8,128)(2,1)} fusion(bf16[4,3000,500,1]{2,1,0,3:T(8,128)(2,1)} %bitcast.59, bf16[2,4,500,512]{2,1,3,0:T(4,128)(2,1)S(1)} %fusion), kind=kOutput, calls=%fused_computation.6.clone.1 | convolution fusion | flops 12291072000 | bytes 22240000 | tf_op jit(solution)/shard_map/cio,pcov->piv/dot_general | solution.py:21
  413.9 27.6 %convolution_convert_fusion = bf16[2,3000,3000]{2,1,0:T(8,128)(2,1)} fusion(bf16[3000,512]{1,0:T(8,128)(2,1)} %all-gather.4.cloned.1.call-done, bf16[2,3000,512]{2,1,0:T(8,128)(2,1)} %fusion.41), kind=kOutput, calls=%fused_computation | convolution fusion | flops 18449999872 | bytes 45216000 | tf_op jit(solution)/shard_map/piv,jv->pij/dot_general | solution.py:24
Async XLA Ops:
  6.5 33.6 %all-gather.4.cloned.1.call-start = ((), (), s32[]{:S(2)}) async-start(), calls=%async_computation | async-start | bytes 3840000 | tf_op jit(solution)/shard_map/all_gather | solution.py:11
  7.3 247.8 %all-gather.6.cloned.1.call-start = ((), (), s32[]{:S(2)}) async-start(), calls=%async_computation.2 | async-start | bytes 15360000 | tf_op jit(solution)/shard_map/all_gather | solution.py:12
  8.0 383.5 %all-reduce.2.cloned.1.call-start = ((), (), s32[]{:S(2)}) async-start(), calls=%async_computation.1 | async-start | bytes 8388608 | tf_op jit(solution)/shard_map/psum | solution.py:18
  274.2 7.9 %copy-start = (f32[2000]{0:T(1024)S(1)}, f32[2000]{0:T(1024)}, u32[]{:S(2)}) copy-start(f32[2000]{0:T(1024)} %param.8) | copy-start | bytes 24004
  274.2 8.0 %copy-start.1 = (f32[512]{0:T(512)S(1)}, f32[512]{0:T(512)}, u32[]{:S(2)}) copy-start(f32[512]{0:T(512)} %param.9) | copy-start | bytes 6148
Sparse Core Ops, SparseCore 0:
  8.9 31.1 all-gather.3
  41.7 213.3 all-gather.5
  282.2 109.3 all-reduce.1
where the time goes:
time: 448 us
  waiting for transfers between devices  329 us (73%)
  matrix products  89.4 us (20%)
  between operations  13.1 us (3%)
  other arithmetic  8.38 us (2%)
  local copies, waits for them, and re-layouts  7.93 us (2%)
    all_gather x1, waiting for transfers between devices, per_device(): occ_parts = lax.all_gather(occ_coeffs, 'col')  189 us
    psum x1, waiting for transfers between devices, per_device(): coupling = lax.psum(part, ('row', 'col'))  107 us
    all_gather x1, waiting for transfers between devices, per_device(): vir_rows = lax.all_gather(vir_coeffs, 'row', axis=1, tiled=True)  32.1 us
    dot_general x1, matrix products, per_device(): jnp.einsum('piv,jv->pij', mixed, vir_rows, preferred_element_type=F32)  27.6 us
    dot_general x1, matrix products, per_device(): jnp.einsum('pij,jv->piv', perturbation, vir_rows, preferred_element_type=...  25.8 us
    dot_general x1, matrix products, per_device(): jnp.einsum('cio,piv->pcov', occ_parts, image, preferred_element_type=F32)  19.1 us
    dot_general x1, matrix products, per_device(): jnp.einsum('cio,pcov->piv', occ_parts, response, preferred_element_type=F32)  16.8 us
  transfers between devices with their start and end apart: 3, of which 3 were waited for; matrix products, arithmetic and copies ran while one was open for 6% of the time, Pallas kernels for 0%

commit v1 on v0

--- a/solution.py
+++ b/solution.py
@@ -8,7 +8,12 @@
 
 
 def per_device(perturbation, occ_coeffs, vir_coeffs, occ_energies, vir_energies):
-    vir_rows = lax.all_gather(vir_coeffs, "row", axis=1, tiled=True)
+    ring = [vir_coeffs]
+    for hop in range(3):
+        ring.append(lax.ppermute(ring[-1], "row", [(dev, (dev + 1) % 4) for dev in range(4)]))
+    vir_rows = jnp.roll(
+        jnp.concatenate(ring[::-1], axis=1), (lax.axis_index("row") + 1) * ring[0].shape[1], axis=1
+    )
     occ_parts = lax.all_gather(occ_coeffs, "col")
     cols, _, width = occ_parts.shape
     image = jnp.einsum("pij,jv->piv", perturbation, vir_rows, preferred_element_type=F32).astype(

time: 448 us -> 416 us (0.929)
  waiting for transfers between devices: 329 us -> 272 us
  local copies, waits for them, and re-layouts: 7.93 us -> 34.5 us
  matrix products: 89.4 us -> 84.6 us
    all_gather x1, waiting for transfers between devices: 189 us -> 133 us  [per_device(): occ_parts = lax.all_gather(occ_coeffs, 'col')]
    ppermute x0 -> x3, waiting for transfers between devices: none -> 34 us  [per_device(): lax.ppermute(ring[-1], 'row', [(dev, (dev + 1) % 4) for dev in range(4)])]
    all_gather x1 -> x0, waiting for transfers between devices: 32.1 us -> none  [per_device(): vir_rows = lax.all_gather(vir_coeffs, 'row', axis=1, tiled=True)]
    unnamed x5 -> x15, local copies, waits for them, and re-layouts: 7.85 us -> 31.1 us
    dot_general x1 -> x0, matrix products: 16.8 us -> none  [per_device(): jnp.einsum('cio,pcov->piv', occ_parts, response, preferred_element_type=F32)]
    dot_general x1, matrix products: 27.6 us -> 39.1 us  [per_device(): jnp.einsum('piv,jv->pij', mixed, vir_rows, preferred_element_type=F32)]
  transfers between devices with their start and end apart: 3 -> 5, of which waited for: 3 -> 5; matrix products, arithmetic and copies ran while one was open for 6% -> 13% of each run, Pallas kernels for 0% -> 0%
where the time goes in v1:
time: 416 us
  waiting for transfers between devices  272 us (65%)
  matrix products  84.6 us (20%)
  local copies, waits for them, and re-layouts  34.5 us (8%)
  between operations  13.4 us (3%)
  other arithmetic  10.6 us (3%)
    all_gather x1, waiting for transfers between devices, per_device(): occ_parts = lax.all_gather(occ_coeffs, 'col')  133 us
    psum x1, waiting for transfers between devices, per_device(): coupling = lax.psum(part, ('row', 'col'))  104 us
    dot_general x1, matrix products, per_device(): jnp.einsum('piv,jv->pij', mixed, vir_rows, preferred_element_type=F32)  39.1 us
    ppermute x3, waiting for transfers between devices, per_device(): lax.ppermute(ring[-1], 'row', [(dev, (dev + 1) % 4) for dev in range(4)])  34 us
    unnamed x15, local copies, waits for them, and re-layouts  31.1 us
    dot_general x1, matrix products, per_device(): jnp.einsum('pij,jv->piv', perturbation, vir_rows, preferred_element_type=...  25.6 us
    dot_general x1, matrix products, per_device(): jnp.einsum('cio,piv->pcov', occ_parts, image, preferred_element_type=F32)  20 us
  transfers between devices with their start and end apart: 5, of which 5 were waited for; matrix products, arithmetic and copies ran while one was open for 13% of the time, Pallas kernels for 0%

profile of v1, /device:TPU:0, one launch (start us, length us, event | category | flops | bytes accessed | tf_op | source)
XLA Modules:
  0.0 415.8 jit_solution(15590853100193963281)
XLA Ops:
  6.5 0.0 copy-start
  6.5 0.0 all-gather.3.cloned.1.call-start
  6.5 0.7 all-gather.3.cloned.1.call-update
  7.3 0.0 all-reduce.2.cloned.1.call-start
  7.3 0.5 collective-permute-start
  7.8 11.6 %collective-permute-done = bf16[3000,128]{1,0:T(8,128)(2,1)S(1)} collective-permute-done((bf16[3000,128]{1,0:T(8,128)(2,1)}, bf16[3000,128]{1,0:T(8,128)(2,1)S(1)}, u32[]{:S(2)}, u32[]{:S(2)}) %collective-permute-start) | collective-permute-done | bytes 768032 | tf_op jit(solution)/shard_map/ppermute | solution.py:13
  19.4 0.0 collective-permute-start.1
  19.5 11.2 %collective-permute-done.1 = bf16[3000,128]{1,0:T(8,128)(2,1)S(1)} collective-permute-done((bf16[3000,128]{1,0:T(8,128)(2,1)S(1)}, bf16[3000,128]{1,0:T(8,128)(2,1)S(1)}, u32[]{:S(2)}, u32[]{:S(2)}) %collective-permute-start.1) | collective-permute-done | bytes 768032 | tf_op jit(solution)/shard_map/ppermute | solution.py:13
  30.7 0.0 collective-permute-start.2
  30.7 11.2 %collective-permute-done.2 = bf16[3000,128]{1,0:T(8,128)(2,1)S(1)} collective-permute-done((bf16[3000,128]{1,0:T(8,128)(2,1)S(1)}, bf16[3000,128]{1,0:T(8,128)(2,1)S(1)}, u32[]{:S(2)}, u32[]{:S(2)}) %collective-permute-start.2) | collective-permute-done | bytes 768032 | tf_op jit(solution)/shard_map/ppermute | solution.py:13
  41.9 1.0 constant_dynamic-update-slice_fusion.7
  42.9 1.0 constant_dynamic-update-slice_fusion.6
  43.9 0.9 constant_dynamic-update-slice_fusion.5
  44.8 0.0 copy-done
  44.8 1.0 constant_dynamic-update-slice_fusion.4
  45.8 1.0 constant_dynamic-update-slice_fusion.3
  46.8 1.0 constant_dynamic-update-slice_fusion.2
  47.8 1.0 constant_dynamic-update-slice_fusion.1
  48.8 1.0 constant_dynamic-update-slice_fusion
  49.8 25.6 %convolution_convert_fusion.1 = bf16[512,2,3000]{0,2,1:T(8,128)(2,1)} fusion(bf16[2,3000,3000]{2,1,0:T(8,128)(2,1)} %param.5, bf16[3000,1024]{1,0:T(8,128)(2,1)} %constant_dynamic-update-slice_fusion, s32[]{:T(128)S(6)} %select_n.14), kind=kOutput, calls=%fused_computation.7 | convolution fusion | flops 18435072000 | bytes 46080004 | tf_op jit(solution)/shard_map/pij,jv->piv/dot_general | solution.py:19
  75.3 16.3 %copy.11 = bf16[512,2,3000]{2,1,0:T(2,128)(2,1)} copy(bf16[512,2,3000]{0,2,1:T(8,128)(2,1)} %convolution_convert_fusion.1) | data formatting | bytes 12288000
  91.7 133.3 %all-gather.3.cloned.1.call-done = bf16[12000,500]{1,0:T(8,128)(2,1)} async-done(((bf16[3000,500]{1,0:T(8,128)(2,1)}), bf16[12000,500]{1,0:T(8,128)(2,1)}) %all-gather.3.cloned.1.call-update) | async-done | bytes 12000016 | tf_op jit(solution)/shard_map/all_gather | solution.py:17
  225.0 20.0 %fusion.13 = bf16[2,512,4,500]{1,3,2,0:T(8,128)(2,1)} fusion(bf16[4,3000,500,1]{2,1,0,3:T(8,128)(2,1)} %bitcast.41, bf16[2,3000,512,1]{1,0,2,3:T(2,128)(2,1)} %bitcast.40), kind=kOutput, calls=%fused_computation.13 | convolution fusion | flops 12290048000 | bytes 22240000 | tf_op jit(solution)/shard_map/cio,piv->pcov/dot_general | solution.py:22
  245.0 0.0 copy-start.1
  245.0 0.0 copy-start.2
  245.0 7.8 %copy.12 = bf16[2,512,4,500]{3,2,1,0:T(4,128)(2,1)} copy(bf16[2,512,4,500]{1,3,2,0:T(8,128)(2,1)} %fusion.13) | data formatting | bytes 8192000
  252.9 0.0 all-reduce.2.cloned.1.call-update
  252.9 0.0 copy-done.1
  252.9 0.1 sub.24
  253.0 0.0 copy-done.2
  253.0 3.1 broadcast_subtract_fusion
  256.1 2.3 fusion.33
  258.4 104.0 %all-reduce.2.cloned.1.call-done = bf16[2,4,500,512]{2,1,3,0:T(4,128)(2,1)} async-done(((bf16[2,4,500,512]{2,1,3,0:T(4,128)(2,1)}), bf16[2,4,500,512]{2,1,3,0:T(4,128)(2,1)}) %all-reduce.2.cloned.1.call-update) | async-done | bytes 4096016 | tf_op jit(solution)/shard_map/psum | solution.py:23
  362.4 7.5 %fusion = bf16[2,4,500,512]{2,1,3,0:T(4,128)(2,1)} fusion(bf16[2,4,500,512]{2,1,3,0:T(4,128)(2,1)} %all-reduce.2.cloned.1.call-done, f32[4,500,512]{1,0,2:T(4,128)} %broadcast_subtract_fusion), kind=kLoop, calls=%fused_computation.3 | loop fusion | flops 6144000 | bytes 12288000 | tf_op jit(solution)/shard_map/convert_element_type | solution.py:25
  369.9 39.1 %convolution_convert_fusion = bf16[2,3000,3000]{2,1,0:T(8,128)(2,1)} fusion(bf16[4,3000,500,1]{2,1,0,3:T(8,128)(2,1)} %bitcast.42, bf16[2,4,500,512]{2,1,3,0:T(4,128)(2,1)} %fusion, bf16[3000,512,1]{1,0,2:T(8,128)(2,1)S(1)} %fusion.33), kind=kOutput, calls=%fused_computation | convolution fusion | flops 30741071872 | bytes 55168000 | tf_op jit(solution)/shard_map/piv,jv->pij/dot_general | solution.py:29
Async XLA Ops:
  6.5 38.3 %copy-start = (bf16[3000,128]{1,0:T(8,128)(2,1)S(1)}, bf16[3000,128]{1,0:T(8,128)(2,1)}, u32[]{:S(2)}) copy-start(bf16[3000,128]{1,0:T(8,128)(2,1)} %param.7) | copy-start | bytes 2304004
  6.5 218.5 %all-gather.3.cloned.1.call-start = ((), (), s32[]{:S(2)}) async-start(), calls=%async_computation.1 | async-start | bytes 15360000 | tf_op jit(solution)/shard_map/all_gather | solution.py:17
  7.3 355.2 %all-reduce.2.cloned.1.call-start = ((), (), s32[]{:S(2)}) async-start(), calls=%async_computation | async-start | bytes 8388608 | tf_op jit(solution)/shard_map/psum | solution.py:23
  7.3 12.1 %collective-permute-start = (bf16[3000,128]{1,0:T(8,128)(2,1)}, bf16[3000,128]{1,0:T(8,128)(2,1)S(1)}, u32[]{:S(2)}, u32[]{:S(2)}) collective-permute-start(bf16[3000,128]{1,0:T(8,128)(2,1)} %param.7), channel_id=1, source_target_pairs={{0,4},{4,8},{8,12},{12,0},{1,5},{5,9},{9,13},{13,1},{2,6},{6,10},{... | collective-permute-start | bytes 2304008 | tf_op jit(solution)/shard_map/ppermute | solution.py:13
  19.4 11.2 %collective-permute-start.1 = (bf16[3000,128]{1,0:T(8,128)(2,1)S(1)}, bf16[3000,128]{1,0:T(8,128)(2,1)S(1)}, u32[]{:S(2)}, u32[]{:S(2)}) collective-permute-start(bf16[3000,128]{1,0:T(8,128)(2,1)S(1)} %collective-permute-done), channel_id=1, source_target_pairs={{0,4},{4,8},{8,12},{12,0},{1,5},{5,9},{9,13},{13,1},{2,6},{6,10},{... | collective-permute-start | bytes 2304008 | tf_op jit(solution)/shard_map/ppermute | solution.py:13
  30.7 11.2 %collective-permute-start.2 = (bf16[3000,128]{1,0:T(8,128)(2,1)S(1)}, bf16[3000,128]{1,0:T(8,128)(2,1)S(1)}, u32[]{:S(2)}, u32[]{:S(2)}) collective-permute-start(bf16[3000,128]{1,0:T(8,128)(2,1)S(1)} %collective-permute-done.1), channel_id=1, source_target_pairs={{0,4},{4,8},{8,12},{12,0},{1,5},{5,9},{9,13},{13,1},{2,6},{6,10},{... | collective-permute-start | bytes 2304008 | tf_op jit(solution)/shard_map/ppermute | solution.py:13
  245.0 7.9 %copy-start.1 = (f32[2000]{0:T(1024)S(1)}, f32[2000]{0:T(1024)}, u32[]{:S(2)}) copy-start(f32[2000]{0:T(1024)} %param.8) | copy-start | bytes 24004
  245.0 8.0 %copy-start.2 = (f32[512]{0:T(512)S(1)}, f32[512]{0:T(512)}, u32[]{:S(2)}) copy-start(f32[512]{0:T(512)} %param.9) | copy-start | bytes 6148
Sparse Core Ops, SparseCore 0:
  8.9 216.0 all-gather.2
  253.0 109.3 all-reduce.1
